TPU v7x, 32 devices: a whole 2x2x4 slice. The times are simulated.
32 devices in a mesh: trial: 4 (over z), south: 2 (over core), east: 2 (over x), down: 2 (over y).
Axes of the slice: x: 2, y: 2, z: 4, core: 2. Of those that a mesh axis runs over, the one named last changes fastest.
Arguments:
- tracer: float32 [32, 32, 256, 128], P(('trial', 'south'), 'east', 'down'), parts along dimension 0, may hold values from 0.5 to 2
- mobility: float32 [32, 32, 256, 128], P(('trial', 'south'), 'east', 'down'), parts along dimension 0, may hold values from 0.03 to 0.15
- source: float32 [32, 32, 256, 128], P(('trial', 'south'), 'east', 'down'), parts along dimension 0, may hold values from -0.2 to 0.2
Outputs:
- standardized: float32 [32, 32, 256, 128], P(('trial', 'south'), 'east', 'down'), parts along dimension 0
- tracer_end: float32 [32, 32, 256, 128], P(('trial', 'south'), 'east', 'down'), parts along dimension 0
There are 4 independent parts, one for each index of `trial`. A program takes and returns all parts, laid end to end along the dimension named above; each array names one. Nothing has to cross between parts.
All inputs are finite; a program needn't handle non-finite values.
Results may differ from a plain program's by a relative error of at most 0.00002.
Values sent between devices are 32-bit elements; how exact they have to be, the bound alone decides.
A program may use at most 128 MiB of HBM per device.

v0:
```python
import jax
import jax.numpy as jnp
from jax import lax
from jax.sharding import PartitionSpec as P

STEPS = 3


def with_halo(block, sides, width):
    for axis, dim in sides:
        count = lax.axis_size(axis)
        forward = [(i, i + 1) for i in range(count - 1)]
        forward.append((count - 1, 0))
        backward = [(target, source) for source, target in forward]
        low = lax.ppermute(
            lax.slice_in_dim(block, block.shape[dim] - width, None, axis=dim), axis, forward
        )
        high = lax.ppermute(lax.slice_in_dim(block, 0, width, axis=dim), axis, backward)
        block = jnp.concatenate([low, block, high], axis=dim)
    return block


def strip_edges(values, dims):
    for dim in dims:
        values = lax.slice_in_dim(values, 1, values.shape[dim] - 1, axis=dim)
    return values


def neighbour(values, dim, start, dims):
    others = [other for other in dims if other != dim]
    values = strip_edges(values, others)
    return lax.slice_in_dim(values, start, start + values.shape[dim] - 2, axis=dim)


def one_step(padded, mobility, source):
    middle = strip_edges(padded, (0, 1, 2))
    lower = [neighbour(padded, dim, 0, (0, 1, 2)) for dim in (0, 1, 2)]
    upper = [neighbour(padded, dim, 2, (0, 1, 2)) for dim in (0, 1, 2)]
    spread = lower[0] + upper[0] + lower[1] + upper[1] + lower[2] + upper[2] - 6.0 * middle
    return middle + mobility * spread + source


def body(tracer, mobility, source):
    for step in range(STEPS):
        padded = with_halo(tracer, (("south", 0), ("east", 1), ("down", 2)), 1)
        tracer = one_step(padded, mobility, source)
    count = tracer.shape[2] * lax.axis_size("down")
    line_mean = lax.psum(jnp.sum(tracer, axis=2, keepdims=True), "down") / count
    centred = tracer - line_mean
    line_variance = lax.psum(jnp.sum(centred * centred, axis=2, keepdims=True), "down") / count
    standardized = centred * lax.rsqrt(line_variance + 0.0001)
    return (standardized, tracer)


def solution(mesh):
    in_specs = (
        P(("trial", "south"), "east", "down", None),
        P(("trial", "south"), "east", "down", None),
        P(("trial", "south"), "east", "down", None),
    )
    out_specs = (
        P(("trial", "south"), "east", "down", None),
        P(("trial", "south"), "east", "down", None),
    )
    return jax.shard_map(body, mesh=mesh, in_specs=in_specs, out_specs=out_specs, check_vma=False)
```

profile of v0, /device:TPU:0, one launch (start us, length us, event | category | flops | bytes accessed | tf_op | source)
XLA Modules:
  0.0 147.4 jit_solution(11715911265367690488)
XLA Ops:
  0.6 0.0 copy-start.3
  0.6 1.8 %fusion.32 = (f32[1,16,128,128]{3,2,1,0:T(8,128)S(1)}, f32[1,16,128,128]{3,2,1,0:T(8,128)S(1)}) fusion(f32[4,16,128,128]{3,2,1,0:T(8,128)} %param.3), kind=kLoop, calls=%fused_computation.103 | loop fusion | bytes 4194304 | tf_op jit(solution)/shard_map/slice | solution.py:18
  2.5 0.6 collective-permute-start
  3.0 0.1 collective-permute-start.1
  3.1 2.2 %collective-permute-done = f32[1,16,128,128]{3,2,1,0:T(8,128)S(1)} collective-permute-done((f32[1,16,128,128]{3,2,1,0:T(8,128)S(1)}, f32[1,16,128,128]{3,2,1,0:T(8,128)S(1)}, u32[]{:S(2)}, u32[]{:S(2)}) %collective-permute-start) | collective-permute-done | bytes 1048608 | tf_op jit(solution)/shard_map/ppermute | solution.py:15
  5.3 0.1 constant_dynamic-update-slice_fusion.2
  5.4 0.0 copy-done.3
  5.4 0.5 constant_dynamic-update-slice_fusion.1
  5.9 0.9 collective-permute-done.1
  6.8 0.1 constant_dynamic-update-slice_fusion
  6.9 0.0 copy-start.2
  6.9 0.0 copy-start
  7.0 0.1 fusion.29
  7.0 2.9 %collective-permute-start.2 = (f32[6,1,128,128]{3,2,1,0:T(8,128)S(1)}, f32[6,1,128,128]{3,2,1,0:T(8,128)S(1)}, u32[]{:S(2)}, u32[]{:S(2)}) collective-permute-start(f32[6,1,128,128]{3,2,1,0:T(8,128)S(1)} %get-tuple-element.14), channel_id=1, source_target_pairs={{0,2},{2,0},{1,3},{3,1},{4,6},{6,4},{5,7},{7,5},{8,10},{10,8},{9,1... | collective-permute-start | bytes 1179656 | tf_op jit(solution)/shard_map/ppermute | solution.py:15
  9.9 0.1 collective-permute-start.3
  10.0 9.9 %collective-permute-done.2 = f32[6,1,128,128]{3,2,1,0:T(8,128)S(1)} collective-permute-done((f32[6,1,128,128]{3,2,1,0:T(8,128)S(1)}, f32[6,1,128,128]{3,2,1,0:T(8,128)S(1)}, u32[]{:S(2)}, u32[]{:S(2)}) %collective-permute-start.2) | collective-permute-done | bytes 393248 | tf_op jit(solution)/shard_map/ppermute | solution.py:15
  19.9 7.9 %collective-permute-done.3 = f32[6,1,128,128]{3,2,1,0:T(8,128)S(1)} collective-permute-done((f32[6,1,128,128]{3,2,1,0:T(8,128)S(1)}, f32[6,1,128,128]{3,2,1,0:T(8,128)S(1)}, u32[]{:S(2)}, u32[]{:S(2)}) %collective-permute-start.3) | collective-permute-done | bytes 393248 | tf_op jit(solution)/shard_map/ppermute | solution.py:18
  27.8 0.1 pad_maximum_fusion.64
  27.9 1.8 %collective-permute-start.4 = (f32[6,18,1,128]{3,2,1,0:T(1,128)S(1)}, f32[6,18,1,128]{3,2,1,0:T(1,128)S(1)}, u32[]{:S(2)}, u32[]{:S(2)}) collective-permute-start(f32[6,18,1,128]{3,2,1,0:T(1,128)S(1)} %get-tuple-element.8), channel_id=1, source_target_pairs={{0,1},{1,0},{2,3},{3,2},{4,5},{5,4},{6,7},{7,6},{8,9},{9,8},{10,11... | collective-permute-start | bytes 165896 | tf_op jit(solution)/shard_map/ppermute | solution.py:15
  29.7 0.3 collective-permute-start.5
  29.9 2.5 %collective-permute-done.4 = f32[6,18,1,128]{3,2,1,0:T(1,128)S(1)} collective-permute-done((f32[6,18,1,128]{3,2,1,0:T(1,128)S(1)}, f32[6,18,1,128]{3,2,1,0:T(1,128)S(1)}, u32[]{:S(2)}, u32[]{:S(2)}) %collective-permute-start.4) | collective-permute-done | bytes 55328 | tf_op jit(solution)/shard_map/ppermute | solution.py:15
  32.5 0.0 copy-done.2
  32.5 1.4 collective-permute-done.5
  33.8 0.0 copy-done
  33.8 13.8 %fusion.22 = f32[4,16,128,128]{3,2,1,0:T(8,128)S(1)} fusion(f32[4,16,128,128]{3,2,1,0:T(8,128)S(1)} %copy-done, f32[4,16,128,128]{3,2,1,0:T(8,128)} %param.3, f32[4,16,128,128]{3,2,1,0:T(8,128)} %param.4, f32[6,18,1,128]{3,2,1,0:T(1,128)S(1)} %collective-permute-done.5, f32[6,1,128,128]{3,2,1,0:T(8,128)S(1)} %collective-permute-done.3, ...), kind=kLoop, calls=%fused_computation.59 | loop fusion | flops 20971520 | bytes 26062848 | tf_op jit(solution)/shard_map/add | solution.py:40
  47.6 0.1 fusion.31
  47.8 0.1 collective-permute-start.6
  47.8 0.5 collective-permute-start.7
  48.3 2.1 %collective-permute-done.6 = f32[1,16,128,128]{3,2,1,0:T(8,128)S(1)} collective-permute-done((f32[1,16,128,128]{3,2,1,0:T(8,128)S(1)}, f32[1,16,128,128]{3,2,1,0:T(8,128)S(1)}, u32[]{:S(2)}, u32[]{:S(2)}) %collective-permute-start.6) | collective-permute-done | bytes 1048608 | tf_op jit(solution)/shard_map/ppermute | solution.py:15
  50.5 1.5 %collective-permute-done.7 = f32[1,16,128,128]{3,2,1,0:T(8,128)S(1)} collective-permute-done((f32[1,16,128,128]{3,2,1,0:T(8,128)S(1)}, f32[1,16,128,128]{3,2,1,0:T(8,128)S(1)}, u32[]{:S(2)}, u32[]{:S(2)}) %collective-permute-start.7) | collective-permute-done | bytes 1048608 | tf_op jit(solution)/shard_map/ppermute | solution.py:18
  52.0 0.1 pad_maximum_fusion.51
  52.1 0.0 copy-start.1
  52.1 1.6 %collective-permute-start.8 = (f32[6,1,128,128]{3,2,1,0:T(8,128)S(1)}, f32[6,1,128,128]{3,2,1,0:T(8,128)S(1)}, u32[]{:S(2)}, u32[]{:S(2)}) collective-permute-start(f32[6,1,128,128]{3,2,1,0:T(8,128)S(1)} %get-tuple-element.12), channel_id=1, source_target_pairs={{0,2},{2,0},{1,3},{3,1},{4,6},{6,4},{5,7},{7,5},{8,10},{10,8},{9,1... | collective-permute-start | bytes 1179656 | tf_op jit(solution)/shard_map/ppermute | solution.py:15
  53.6 0.5 collective-permute-start.9
  54.2 10.0 %collective-permute-done.8 = f32[6,1,128,128]{3,2,1,0:T(8,128)S(1)} collective-permute-done((f32[6,1,128,128]{3,2,1,0:T(8,128)S(1)}, f32[6,1,128,128]{3,2,1,0:T(8,128)S(1)}, u32[]{:S(2)}, u32[]{:S(2)}) %collective-permute-start.8) | collective-permute-done | bytes 393248 | tf_op jit(solution)/shard_map/ppermute | solution.py:15
  64.1 7.6 %collective-permute-done.9 = f32[6,1,128,128]{3,2,1,0:T(8,128)S(1)} collective-permute-done((f32[6,1,128,128]{3,2,1,0:T(8,128)S(1)}, f32[6,1,128,128]{3,2,1,0:T(8,128)S(1)}, u32[]{:S(2)}, u32[]{:S(2)}) %collective-permute-start.9) | collective-permute-done | bytes 393248 | tf_op jit(solution)/shard_map/ppermute | solution.py:18
  71.7 0.1 pad_maximum_fusion.61
  71.8 0.7 collective-permute-start.10
  72.5 1.4 collective-permute-start.11
  73.9 2.1 %collective-permute-done.10 = f32[6,18,1,128]{3,2,1,0:T(1,128)S(1)} collective-permute-done((f32[6,18,1,128]{3,2,1,0:T(1,128)S(1)}, f32[6,18,1,128]{3,2,1,0:T(1,128)S(1)}, u32[]{:S(2)}, u32[]{:S(2)}) %collective-permute-start.10) | collective-permute-done | bytes 55328 | tf_op jit(solution)/shard_map/ppermute | solution.py:15
  76.0 0.6 collective-permute-done.11
  76.6 0.0 copy-done.1
  76.6 7.6 %fusion.13 = f32[4,16,128,128]{3,2,1,0:T(8,128)S(1)} fusion(f32[4,16,128,128]{3,2,1,0:T(8,128)S(1)} %copy-done, f32[4,16,128,128]{3,2,1,0:T(8,128)S(1)} %fusion.22, f32[4,16,128,128]{3,2,1,0:T(8,128)S(1)} %copy-done.1, f32[6,18,1,128]{3,2,1,0:T(1,128)S(1)} %collective-permute-done.11, f32[6,1,128,128]{3,2,1,0:T(8,128)S(1)} %collective-permute-done.9, ...), kind=kLoop, calls=%fused_computation.32 | loop fusion | flops 29360128 | bytes 19771392 | tf_op jit(solution)/shard_map/add | solution.py:40
  84.2 0.2 fusion.30
  84.4 0.1 collective-permute-start.12
  84.5 0.5 collective-permute-start.13
  85.0 2.1 %collective-permute-done.12 = f32[1,16,128,128]{3,2,1,0:T(8,128)S(1)} collective-permute-done((f32[1,16,128,128]{3,2,1,0:T(8,128)S(1)}, f32[1,16,128,128]{3,2,1,0:T(8,128)S(1)}, u32[]{:S(2)}, u32[]{:S(2)}) %collective-permute-start.12) | collective-permute-done | bytes 1048608 | tf_op jit(solution)/shard_map/ppermute | solution.py:15
  87.2 1.5 %collective-permute-done.13 = f32[1,16,128,128]{3,2,1,0:T(8,128)S(1)} collective-permute-done((f32[1,16,128,128]{3,2,1,0:T(8,128)S(1)}, f32[1,16,128,128]{3,2,1,0:T(8,128)S(1)}, u32[]{:S(2)}, u32[]{:S(2)}) %collective-permute-start.13) | collective-permute-done | bytes 1048608 | tf_op jit(solution)/shard_map/ppermute | solution.py:18
  88.7 0.1 pad_maximum_fusion.48
  88.7 1.6 %collective-permute-start.14 = (f32[6,1,128,128]{3,2,1,0:T(8,128)S(1)}, f32[6,1,128,128]{3,2,1,0:T(8,128)S(1)}, u32[]{:S(2)}, u32[]{:S(2)}) collective-permute-start(f32[6,1,128,128]{3,2,1,0:T(8,128)S(1)} %get-tuple-element.10), channel_id=1, source_target_pairs={{0,2},{2,0},{1,3},{3,1},{4,6},{6,4},{5,7},{7,5},{8,10},{10,8},{9,1... | collective-permute-start | bytes 1179656 | tf_op jit(solution)/shard_map/ppermute | solution.py:15
  90.3 0.5 collective-permute-start.15
  90.8 10.0 %collective-permute-done.14 = f32[6,1,128,128]{3,2,1,0:T(8,128)S(1)} collective-permute-done((f32[6,1,128,128]{3,2,1,0:T(8,128)S(1)}, f32[6,1,128,128]{3,2,1,0:T(8,128)S(1)}, u32[]{:S(2)}, u32[]{:S(2)}) %collective-permute-start.14) | collective-permute-done | bytes 393248 | tf_op jit(solution)/shard_map/ppermute | solution.py:15
  100.8 7.6 %collective-permute-done.15 = f32[6,1,128,128]{3,2,1,0:T(8,128)S(1)} collective-permute-done((f32[6,1,128,128]{3,2,1,0:T(8,128)S(1)}, f32[6,1,128,128]{3,2,1,0:T(8,128)S(1)}, u32[]{:S(2)}, u32[]{:S(2)}) %collective-permute-start.15) | collective-permute-done | bytes 393248 | tf_op jit(solution)/shard_map/ppermute | solution.py:18
  108.4 0.1 pad_maximum_fusion.56
  108.4 1.5 %collective-permute-start.16 = (f32[6,18,1,128]{3,2,1,0:T(1,128)S(1)}, f32[6,18,1,128]{3,2,1,0:T(1,128)S(1)}, u32[]{:S(2)}, u32[]{:S(2)}) collective-permute-start(f32[6,18,1,128]{3,2,1,0:T(1,128)S(1)} %get-tuple-element.4), channel_id=1, source_target_pairs={{0,1},{1,0},{2,3},{3,2},{4,5},{5,4},{6,7},{7,6},{8,9},{9,8},{10,11... | collective-permute-start | bytes 165896 | tf_op jit(solution)/shard_map/ppermute | solution.py:15
  109.9 0.6 collective-permute-start.17
  110.5 2.2 %collective-permute-done.16 = f32[6,18,1,128]{3,2,1,0:T(1,128)S(1)} collective-permute-done((f32[6,18,1,128]{3,2,1,0:T(1,128)S(1)}, f32[6,18,1,128]{3,2,1,0:T(1,128)S(1)}, u32[]{:S(2)}, u32[]{:S(2)}) %collective-permute-start.16) | collective-permute-done | bytes 55328 | tf_op jit(solution)/shard_map/ppermute | solution.py:15
  112.7 1.4 collective-permute-done.17
  114.1 9.3 %fusion.27 = (f32[4,16,128]{2,1,0:T(8,128)S(1)}, f32[4,16,128,128]{3,2,1,0:T(8,128)}) fusion(f32[4,16,128,128]{3,2,1,0:T(8,128)S(1)} %copy-done, f32[4,16,128,128]{3,2,1,0:T(8,128)S(1)} %fusion.13, f32[4,16,128,128]{3,2,1,0:T(8,128)S(1)} %copy-done.1, f32[6,18,1,128]{3,2,1,0:T(1,128)S(1)} %collective-permute-done.17, ...), kind=kLoop, calls=%fused_computation.99 | loop fusion | flops 30400512 | bytes 19804160 | tf_op jit(solution)/shard_map/reduce_sum | solution.py:48
  123.4 7.4 %psum.14 = f32[4,16,1,128]{3,1,0,2:T(8,128)S(1)} all-reduce(f32[4,16,1,128]{3,1,0,2:T(8,128)S(1)} %bitcast.6), channel_id=1, replica_groups=mesh['trial'=4,'south'=2,'east'=2,'down'=2] {'down'}, use_global_device_ids=true, to_apply=%region_1.0 | all-reduce | flops 8192 | bytes 65536 | tf_op jit(solution)/shard_map/psum | solution.py:48
  130.8 3.0 %multiply_reduce_fusion = f32[4,16,128]{2,1,0:T(8,128)S(1)} fusion(f32[4,16,128,128]{3,2,1,0:T(8,128)} %get-tuple-element.3, f32[4,16,128]{2,1,0:T(8,128)S(1)} %multiply_bitcast_fusion), kind=kLoop, calls=%fused_computation.73 | loop fusion | flops 3137536 | bytes 4259840 | tf_op jit(solution)/shard_map/reduce_sum | solution.py:50
  133.8 8.3 %psum.15 = f32[4,16,1,128]{3,1,0,2:T(8,128)S(1)} all-reduce(f32[4,16,1,128]{3,1,0,2:T(8,128)S(1)} %bitcast.7), channel_id=1, replica_groups=mesh['trial'=4,'south'=2,'east'=2,'down'=2] {'down'}, use_global_device_ids=true, to_apply=%region_3.0 | all-reduce | flops 8192 | bytes 65536 | tf_op jit(solution)/shard_map/psum | solution.py:50
  142.1 5.2 %subtract_multiply_fusion = f32[4,16,128,128]{3,2,1,0:T(8,128)} fusion(f32[4,16,128,128]{3,2,1,0:T(8,128)} %get-tuple-element.3, f32[4,16,128]{2,1,0:T(8,128)S(1)} %rsqrt_bitcast_fusion, f32[4,16,128]{2,1,0:T(8,128)S(1)} %multiply_bitcast_fusion), kind=kLoop, calls=%fused_computation.74 | loop fusion | flops 2097152 | bytes 8454144 | tf_op jit(solution)/shard_map/mul | solution.py:51
  (2 shorter events, 0.0 us)
Async XLA Ops:
  0.6 4.8 %copy-start.3 = (f32[4,16,128,128]{3,2,1,0:T(8,128)S(1)}, f32[4,16,128,128]{3,2,1,0:T(8,128)}, u32[]{:S(2)}) copy-start(f32[4,16,128,128]{3,2,1,0:T(8,128)} %param.3) | copy-start | bytes 12582916
  2.5 2.8 %collective-permute-start = (f32[1,16,128,128]{3,2,1,0:T(8,128)S(1)}, f32[1,16,128,128]{3,2,1,0:T(8,128)S(1)}, u32[]{:S(2)}, u32[]{:S(2)}) collective-permute-start(f32[1,16,128,128]{3,2,1,0:T(8,128)S(1)} %get-tuple-element.21), channel_id=1, source_target_pairs={{0,4},{4,0},{1,5},{5,1},{2,6},{6,2},{3,7},{7,3},{8,12},{12,8},{9,1... | collective-permute-start | bytes 3145736 | tf_op jit(solution)/shard_map/ppermute | solution.py:15
  3.0 3.8 %collective-permute-start.1 = (f32[1,16,128,128]{3,2,1,0:T(8,128)S(1)}, f32[1,16,128,128]{3,2,1,0:T(8,128)S(1)}, u32[]{:S(2)}, u32[]{:S(2)}) collective-permute-start(f32[1,16,128,128]{3,2,1,0:T(8,128)S(1)} %get-tuple-element.20), channel_id=1, source_target_pairs={{4,0},{0,4},{5,1},{1,5},{6,2},{2,6},{7,3},{3,7},{12,8},{8,12},{13,... | collective-permute-start | bytes 3145736 | tf_op jit(solution)/shard_map/ppermute | solution.py:18
  6.9 25.5 %copy-start.2 = (f32[6,16,128,128]{3,2,1,0:T(8,128)}, f32[6,16,128,128]{3,2,1,0:T(8,128)S(1)}, u32[]{:S(2)}) copy-start(f32[6,16,128,128]{3,2,1,0:T(8,128)S(1)} %constant_dynamic-update-slice_fusion) | copy-start | bytes 18874372
  6.9 26.9 %copy-start = (f32[4,16,128,128]{3,2,1,0:T(8,128)S(1)}, f32[4,16,128,128]{3,2,1,0:T(8,128)}, u32[]{:S(2)}) copy-start(f32[4,16,128,128]{3,2,1,0:T(8,128)} %param.5) | copy-start | bytes 12582916
  7.0 12.9 %collective-permute-start.2 = (f32[6,1,128,128]{3,2,1,0:T(8,128)S(1)}, f32[6,1,128,128]{3,2,1,0:T(8,128)S(1)}, u32[]{:S(2)}, u32[]{:S(2)}) collective-permute-start(f32[6,1,128,128]{3,2,1,0:T(8,128)S(1)} %get-tuple-element.14), channel_id=1, source_target_pairs={{0,2},{2,0},{1,3},{3,1},{4,6},{6,4},{5,7},{7,5},{8,10},{10,8},{9,1... | collective-permute-start | bytes 1179656 | tf_op jit(solution)/shard_map/ppermute | solution.py:15
  9.9 17.8 %collective-permute-start.3 = (f32[6,1,128,128]{3,2,1,0:T(8,128)S(1)}, f32[6,1,128,128]{3,2,1,0:T(8,128)S(1)}, u32[]{:S(2)}, u32[]{:S(2)}) collective-permute-start(f32[6,1,128,128]{3,2,1,0:T(8,128)S(1)} %get-tuple-element.15), channel_id=1, source_target_pairs={{2,0},{0,2},{3,1},{1,3},{6,4},{4,6},{7,5},{5,7},{10,8},{8,10},{11,... | collective-permute-start | bytes 1179656 | tf_op jit(solution)/shard_map/ppermute | solution.py:18
  27.9 4.6 %collective-permute-start.4 = (f32[6,18,1,128]{3,2,1,0:T(1,128)S(1)}, f32[6,18,1,128]{3,2,1,0:T(1,128)S(1)}, u32[]{:S(2)}, u32[]{:S(2)}) collective-permute-start(f32[6,18,1,128]{3,2,1,0:T(1,128)S(1)} %get-tuple-element.8), channel_id=1, source_target_pairs={{0,1},{1,0},{2,3},{3,2},{4,5},{5,4},{6,7},{7,6},{8,9},{9,8},{10,11... | collective-permute-start | bytes 165896 | tf_op jit(solution)/shard_map/ppermute | solution.py:15
  29.7 4.2 %collective-permute-start.5 = (f32[6,18,1,128]{3,2,1,0:T(1,128)S(1)}, f32[6,18,1,128]{3,2,1,0:T(1,128)S(1)}, u32[]{:S(2)}, u32[]{:S(2)}) collective-permute-start(f32[6,18,1,128]{3,2,1,0:T(1,128)S(1)} %get-tuple-element.9), channel_id=1, source_target_pairs={{1,0},{0,1},{3,2},{2,3},{5,4},{4,5},{7,6},{6,7},{9,8},{8,9},{11,10... | collective-permute-start | bytes 165896 | tf_op jit(solution)/shard_map/ppermute | solution.py:18
  47.8 2.7 %collective-permute-start.6 = (f32[1,16,128,128]{3,2,1,0:T(8,128)S(1)}, f32[1,16,128,128]{3,2,1,0:T(8,128)S(1)}, u32[]{:S(2)}, u32[]{:S(2)}) collective-permute-start(f32[1,16,128,128]{3,2,1,0:T(8,128)S(1)} %get-tuple-element.18), channel_id=1, source_target_pairs={{0,4},{4,0},{1,5},{5,1},{2,6},{6,2},{3,7},{7,3},{8,12},{12,8},{9,1... | collective-permute-start | bytes 3145736 | tf_op jit(solution)/shard_map/ppermute | solution.py:15
  47.8 4.1 %collective-permute-start.7 = (f32[1,16,128,128]{3,2,1,0:T(8,128)S(1)}, f32[1,16,128,128]{3,2,1,0:T(8,128)S(1)}, u32[]{:S(2)}, u32[]{:S(2)}) collective-permute-start(f32[1,16,128,128]{3,2,1,0:T(8,128)S(1)} %get-tuple-element.19), channel_id=1, source_target_pairs={{4,0},{0,4},{5,1},{1,5},{6,2},{2,6},{7,3},{3,7},{12,8},{8,12},{13,... | collective-permute-start | bytes 3145736 | tf_op jit(solution)/shard_map/ppermute | solution.py:18
  52.1 24.6 %copy-start.1 = (f32[4,16,128,128]{3,2,1,0:T(8,128)S(1)}, f32[4,16,128,128]{3,2,1,0:T(8,128)}, u32[]{:S(2)}) copy-start(f32[4,16,128,128]{3,2,1,0:T(8,128)} %param.4) | copy-start | bytes 12582916
  52.1 12.1 %collective-permute-start.8 = (f32[6,1,128,128]{3,2,1,0:T(8,128)S(1)}, f32[6,1,128,128]{3,2,1,0:T(8,128)S(1)}, u32[]{:S(2)}, u32[]{:S(2)}) collective-permute-start(f32[6,1,128,128]{3,2,1,0:T(8,128)S(1)} %get-tuple-element.12), channel_id=1, source_target_pairs={{0,2},{2,0},{1,3},{3,1},{4,6},{6,4},{5,7},{7,5},{8,10},{10,8},{9,1... | collective-permute-start | bytes 1179656 | tf_op jit(solution)/shard_map/ppermute | solution.py:15
  53.6 18.1 %collective-permute-start.9 = (f32[6,1,128,128]{3,2,1,0:T(8,128)S(1)}, f32[6,1,128,128]{3,2,1,0:T(8,128)S(1)}, u32[]{:S(2)}, u32[]{:S(2)}) collective-permute-start(f32[6,1,128,128]{3,2,1,0:T(8,128)S(1)} %get-tuple-element.13), channel_id=1, source_target_pairs={{2,0},{0,2},{3,1},{1,3},{6,4},{4,6},{7,5},{5,7},{10,8},{8,10},{11,... | collective-permute-start | bytes 1179656 | tf_op jit(solution)/shard_map/ppermute | solution.py:18
  71.8 4.2 %collective-permute-start.10 = (f32[6,18,1,128]{3,2,1,0:T(1,128)S(1)}, f32[6,18,1,128]{3,2,1,0:T(1,128)S(1)}, u32[]{:S(2)}, u32[]{:S(2)}) collective-permute-start(f32[6,18,1,128]{3,2,1,0:T(1,128)S(1)} %get-tuple-element.6), channel_id=1, source_target_pairs={{0,1},{1,0},{2,3},{3,2},{4,5},{5,4},{6,7},{7,6},{8,9},{9,8},{10,11... | collective-permute-start | bytes 165896 | tf_op jit(solution)/shard_map/ppermute | solution.py:15
  72.5 4.2 %collective-permute-start.11 = (f32[6,18,1,128]{3,2,1,0:T(1,128)S(1)}, f32[6,18,1,128]{3,2,1,0:T(1,128)S(1)}, u32[]{:S(2)}, u32[]{:S(2)}) collective-permute-start(f32[6,18,1,128]{3,2,1,0:T(1,128)S(1)} %get-tuple-element.7), channel_id=1, source_target_pairs={{1,0},{0,1},{3,2},{2,3},{5,4},{4,5},{7,6},{6,7},{9,8},{8,9},{11,10... | collective-permute-start | bytes 165896 | tf_op jit(solution)/shard_map/ppermute | solution.py:18
  84.4 2.7 %collective-permute-start.12 = (f32[1,16,128,128]{3,2,1,0:T(8,128)S(1)}, f32[1,16,128,128]{3,2,1,0:T(8,128)S(1)}, u32[]{:S(2)}, u32[]{:S(2)}) collective-permute-start(f32[1,16,128,128]{3,2,1,0:T(8,128)S(1)} %get-tuple-element.16), channel_id=1, source_target_pairs={{0,4},{4,0},{1,5},{5,1},{2,6},{6,2},{3,7},{7,3},{8,12},{12,8},{9,1... | collective-permute-start | bytes 3145736 | tf_op jit(solution)/shard_map/ppermute | solution.py:15
  84.5 4.1 %collective-permute-start.13 = (f32[1,16,128,128]{3,2,1,0:T(8,128)S(1)}, f32[1,16,128,128]{3,2,1,0:T(8,128)S(1)}, u32[]{:S(2)}, u32[]{:S(2)}) collective-permute-start(f32[1,16,128,128]{3,2,1,0:T(8,128)S(1)} %get-tuple-element.17), channel_id=1, source_target_pairs={{4,0},{0,4},{5,1},{1,5},{6,2},{2,6},{7,3},{3,7},{12,8},{8,12},{13,... | collective-permute-start | bytes 3145736 | tf_op jit(solution)/shard_map/ppermute | solution.py:18
  88.7 12.1 %collective-permute-start.14 = (f32[6,1,128,128]{3,2,1,0:T(8,128)S(1)}, f32[6,1,128,128]{3,2,1,0:T(8,128)S(1)}, u32[]{:S(2)}, u32[]{:S(2)}) collective-permute-start(f32[6,1,128,128]{3,2,1,0:T(8,128)S(1)} %get-tuple-element.10), channel_id=1, source_target_pairs={{0,2},{2,0},{1,3},{3,1},{4,6},{6,4},{5,7},{7,5},{8,10},{10,8},{9,1... | collective-permute-start | bytes 1179656 | tf_op jit(solution)/shard_map/ppermute | solution.py:15
  90.3 18.1 %collective-permute-start.15 = (f32[6,1,128,128]{3,2,1,0:T(8,128)S(1)}, f32[6,1,128,128]{3,2,1,0:T(8,128)S(1)}, u32[]{:S(2)}, u32[]{:S(2)}) collective-permute-start(f32[6,1,128,128]{3,2,1,0:T(8,128)S(1)} %get-tuple-element.11), channel_id=1, source_target_pairs={{2,0},{0,2},{3,1},{1,3},{6,4},{4,6},{7,5},{5,7},{10,8},{8,10},{11,... | collective-permute-start | bytes 1179656 | tf_op jit(solution)/shard_map/ppermute | solution.py:18
  108.4 4.3 %collective-permute-start.16 = (f32[6,18,1,128]{3,2,1,0:T(1,128)S(1)}, f32[6,18,1,128]{3,2,1,0:T(1,128)S(1)}, u32[]{:S(2)}, u32[]{:S(2)}) collective-permute-start(f32[6,18,1,128]{3,2,1,0:T(1,128)S(1)} %get-tuple-element.4), channel_id=1, source_target_pairs={{0,1},{1,0},{2,3},{3,2},{4,5},{5,4},{6,7},{7,6},{8,9},{9,8},{10,11... | collective-permute-start | bytes 165896 | tf_op jit(solution)/shard_map/ppermute | solution.py:15
  109.9 4.2 %collective-permute-start.17 = (f32[6,18,1,128]{3,2,1,0:T(1,128)S(1)}, f32[6,18,1,128]{3,2,1,0:T(1,128)S(1)}, u32[]{:S(2)}, u32[]{:S(2)}) collective-permute-start(f32[6,18,1,128]{3,2,1,0:T(1,128)S(1)} %get-tuple-element.5), channel_id=1, source_target_pairs={{1,0},{0,1},{3,2},{2,3},{5,4},{4,5},{7,6},{6,7},{9,8},{8,9},{11,10... | collective-permute-start | bytes 165896 | tf_op jit(solution)/shard_map/ppermute | solution.py:18
where the time goes:
time: 148 us; the launch traced here: 147 us
  waiting for transfers between devices  73.5 us (50%)
  other arithmetic  39.2 us (26%)
  blocking collectives  15.7 us (11%)
  starting transfers between devices  15.2 us (10%)
  local copies, waits for them, and re-layouts  2.94 us (2%)
    ppermute x9, waiting for transfers between devices, with_halo(): lax.ppermute(lax.slice_in_dim(block, block.shape[dim] - width, None, axis...  43.1 us
    ppermute x9, waiting for transfers between devices, with_halo(): lax.ppermute(lax.slice_in_dim(block, 0, width, axis=dim), axis, backward)  30.3 us
    add x2, other arithmetic, one_step(): return middle + mobility * spread + source  21.3 us
    ppermute x9, starting transfers between devices, with_halo(): lax.ppermute(lax.slice_in_dim(block, block.shape[dim] - width, None, axis...  10.7 us
    reduce_sum x1, other arithmetic, body(): line_mean = lax.psum(jnp.sum(tracer, axis=2, keepdims=True), 'down') / count  9.27 us
    psum x1, blocking collectives, body(): lax.psum(jnp.sum(centred * centred, axis=2, keepdims=True), 'down') / count  8.28 us
    psum x1, blocking collectives, body(): line_mean = lax.psum(jnp.sum(tracer, axis=2, keepdims=True), 'down') / count  7.43 us
    mul x2, other arithmetic, body(): standardized = centred * lax.rsqrt(line_variance + 0.0001)  5.24 us
  transfers between devices with their start and end apart: 18, of which 18 were waited for; matrix products, arithmetic and copies ran while one was open for 0% of the time, Pallas kernels for 0%

commit v1 on v0

--- a/solution.py
+++ b/solution.py
@@ -47,7 +47,10 @@
     count = tracer.shape[2] * lax.axis_size("down")
     line_mean = lax.psum(jnp.sum(tracer, axis=2, keepdims=True), "down") / count
     centred = tracer - line_mean
-    line_variance = lax.psum(jnp.sum(centred * centred, axis=2, keepdims=True), "down") / count
+    line_variance = (
+        lax.all_gather(jnp.sum(centred * centred, axis=2, keepdims=True), "down").sum(axis=0)
+        / count
+    )
     standardized = centred * lax.rsqrt(line_variance + 0.0001)
     return (standardized, tracer)
 

time: 148 us -> 144 us (0.973)
  blocking collectives: 15.7 us -> 12 us
    psum x1 -> x0, blocking collectives: 8.28 us -> none  [body(): lax.psum(jnp.sum(centred * centred, axis=2, keepdims=True), 'down') / count]
    all_gather x0 -> x1, blocking collectives: none -> 4.58 us  [body(): lax.all_gather(jnp.sum(centred * centred, axis=2, keepdims=True), 'down')]
    mul x2 -> x1, other arithmetic: 5.24 us -> 5.23 us  [body(): standardized = centred * lax.rsqrt(line_variance + 0.0001)]
where the time goes in v1:
time: 144 us
  waiting for transfers between devices  73.5 us (51%)
  other arithmetic  39.2 us (27%)
  starting transfers between devices  15.2 us (11%)
  blocking collectives  12 us (8%)
  local copies, waits for them, and re-layouts  2.94 us (2%)
    ppermute x9, waiting for transfers between devices, with_halo(): lax.ppermute(lax.slice_in_dim(block, block.shape[dim] - width, None, axis...  43.1 us
    ppermute x9, waiting for transfers between devices, with_halo(): lax.ppermute(lax.slice_in_dim(block, 0, width, axis=dim), axis, backward)  30.3 us
    add x2, other arithmetic, one_step(): return middle + mobility * spread + source  21.3 us
    ppermute x9, starting transfers between devices, with_halo(): lax.ppermute(lax.slice_in_dim(block, block.shape[dim] - width, None, axis...  10.7 us
    reduce_sum x1, other arithmetic, body(): line_mean = lax.psum(jnp.sum(tracer, axis=2, keepdims=True), 'down') / count  9.27 us
    psum x1, blocking collectives, body(): line_mean = lax.psum(jnp.sum(tracer, axis=2, keepdims=True), 'down') / count  7.43 us
    mul x1, other arithmetic, body(): standardized = centred * lax.rsqrt(line_variance + 0.0001)  5.23 us
    all_gather x1, blocking collectives, body(): lax.all_gather(jnp.sum(centred * centred, axis=2, keepdims=True), 'down')  4.58 us
  transfers between devices with their start and end apart: 18, of which 18 were waited for; matrix products, arithmetic and copies ran while one was open for 0% of the time, Pallas kernels for 0%

profile of v1, /device:TPU:0, one launch (start us, length us, event | category | flops | bytes accessed | tf_op | source)
XLA Modules:
  0.0 143.6 jit_solution(6873449629453028008)
XLA Ops:
  0.6 0.0 copy-start.3
  0.6 1.8 %fusion.32 = (f32[1,16,128,128]{3,2,1,0:T(8,128)S(1)}, f32[1,16,128,128]{3,2,1,0:T(8,128)S(1)}) fusion(f32[4,16,128,128]{3,2,1,0:T(8,128)} %param.3), kind=kLoop, calls=%fused_computation.103 | loop fusion | bytes 4194304 | tf_op jit(solution)/shard_map/slice | solution.py:18
  2.5 0.6 collective-permute-start
  3.0 0.1 collective-permute-start.1
  3.1 2.2 %collective-permute-done = f32[1,16,128,128]{3,2,1,0:T(8,128)S(1)} collective-permute-done((f32[1,16,128,128]{3,2,1,0:T(8,128)S(1)}, f32[1,16,128,128]{3,2,1,0:T(8,128)S(1)}, u32[]{:S(2)}, u32[]{:S(2)}) %collective-permute-start) | collective-permute-done | bytes 1048608 | tf_op jit(solution)/shard_map/ppermute | solution.py:15
  5.3 0.1 constant_dynamic-update-slice_fusion.2
  5.4 0.0 copy-done.3
  5.4 0.5 constant_dynamic-update-slice_fusion.1
  5.9 0.9 collective-permute-done.1
  6.8 0.1 constant_dynamic-update-slice_fusion
  6.9 0.0 copy-start.2
  6.9 0.0 copy-start
  7.0 0.1 fusion.29
  7.0 2.9 %collective-permute-start.2 = (f32[6,1,128,128]{3,2,1,0:T(8,128)S(1)}, f32[6,1,128,128]{3,2,1,0:T(8,128)S(1)}, u32[]{:S(2)}, u32[]{:S(2)}) collective-permute-start(f32[6,1,128,128]{3,2,1,0:T(8,128)S(1)} %get-tuple-element.14), channel_id=1, source_target_pairs={{0,2},{2,0},{1,3},{3,1},{4,6},{6,4},{5,7},{7,5},{8,10},{10,8},{9,1... | collective-permute-start | bytes 1179656 | tf_op jit(solution)/shard_map/ppermute | solution.py:15
  9.9 0.1 collective-permute-start.3
  10.0 9.9 %collective-permute-done.2 = f32[6,1,128,128]{3,2,1,0:T(8,128)S(1)} collective-permute-done((f32[6,1,128,128]{3,2,1,0:T(8,128)S(1)}, f32[6,1,128,128]{3,2,1,0:T(8,128)S(1)}, u32[]{:S(2)}, u32[]{:S(2)}) %collective-permute-start.2) | collective-permute-done | bytes 393248 | tf_op jit(solution)/shard_map/ppermute | solution.py:15
  19.9 7.9 %collective-permute-done.3 = f32[6,1,128,128]{3,2,1,0:T(8,128)S(1)} collective-permute-done((f32[6,1,128,128]{3,2,1,0:T(8,128)S(1)}, f32[6,1,128,128]{3,2,1,0:T(8,128)S(1)}, u32[]{:S(2)}, u32[]{:S(2)}) %collective-permute-start.3) | collective-permute-done | bytes 393248 | tf_op jit(solution)/shard_map/ppermute | solution.py:18
  27.8 0.1 pad_maximum_fusion.64
  27.9 1.8 %collective-permute-start.4 = (f32[6,18,1,128]{3,2,1,0:T(1,128)S(1)}, f32[6,18,1,128]{3,2,1,0:T(1,128)S(1)}, u32[]{:S(2)}, u32[]{:S(2)}) collective-permute-start(f32[6,18,1,128]{3,2,1,0:T(1,128)S(1)} %get-tuple-element.8), channel_id=1, source_target_pairs={{0,1},{1,0},{2,3},{3,2},{4,5},{5,4},{6,7},{7,6},{8,9},{9,8},{10,11... | collective-permute-start | bytes 165896 | tf_op jit(solution)/shard_map/ppermute | solution.py:15
  29.7 0.3 collective-permute-start.5
  29.9 2.5 %collective-permute-done.4 = f32[6,18,1,128]{3,2,1,0:T(1,128)S(1)} collective-permute-done((f32[6,18,1,128]{3,2,1,0:T(1,128)S(1)}, f32[6,18,1,128]{3,2,1,0:T(1,128)S(1)}, u32[]{:S(2)}, u32[]{:S(2)}) %collective-permute-start.4) | collective-permute-done | bytes 55328 | tf_op jit(solution)/shard_map/ppermute | solution.py:15
  32.5 0.0 copy-done.2
  32.5 1.4 collective-permute-done.5
  33.8 0.0 copy-done
  33.8 13.8 %fusion.22 = f32[4,16,128,128]{3,2,1,0:T(8,128)S(1)} fusion(f32[4,16,128,128]{3,2,1,0:T(8,128)S(1)} %copy-done, f32[4,16,128,128]{3,2,1,0:T(8,128)} %param.3, f32[4,16,128,128]{3,2,1,0:T(8,128)} %param.4, f32[6,18,1,128]{3,2,1,0:T(1,128)S(1)} %collective-permute-done.5, f32[6,1,128,128]{3,2,1,0:T(8,128)S(1)} %collective-permute-done.3, ...), kind=kLoop, calls=%fused_computation.59 | loop fusion | flops 20971520 | bytes 26062848 | tf_op jit(solution)/shard_map/add | solution.py:40
  47.6 0.1 fusion.31
  47.8 0.1 collective-permute-start.6
  47.8 0.5 collective-permute-start.7
  48.3 2.1 %collective-permute-done.6 = f32[1,16,128,128]{3,2,1,0:T(8,128)S(1)} collective-permute-done((f32[1,16,128,128]{3,2,1,0:T(8,128)S(1)}, f32[1,16,128,128]{3,2,1,0:T(8,128)S(1)}, u32[]{:S(2)}, u32[]{:S(2)}) %collective-permute-start.6) | collective-permute-done | bytes 1048608 | tf_op jit(solution)/shard_map/ppermute | solution.py:15
  50.5 1.5 %collective-permute-done.7 = f32[1,16,128,128]{3,2,1,0:T(8,128)S(1)} collective-permute-done((f32[1,16,128,128]{3,2,1,0:T(8,128)S(1)}, f32[1,16,128,128]{3,2,1,0:T(8,128)S(1)}, u32[]{:S(2)}, u32[]{:S(2)}) %collective-permute-start.7) | collective-permute-done | bytes 1048608 | tf_op jit(solution)/shard_map/ppermute | solution.py:18
  52.0 0.1 pad_maximum_fusion.51
  52.1 0.0 copy-start.1
  52.1 1.6 %collective-permute-start.8 = (f32[6,1,128,128]{3,2,1,0:T(8,128)S(1)}, f32[6,1,128,128]{3,2,1,0:T(8,128)S(1)}, u32[]{:S(2)}, u32[]{:S(2)}) collective-permute-start(f32[6,1,128,128]{3,2,1,0:T(8,128)S(1)} %get-tuple-element.12), channel_id=1, source_target_pairs={{0,2},{2,0},{1,3},{3,1},{4,6},{6,4},{5,7},{7,5},{8,10},{10,8},{9,1... | collective-permute-start | bytes 1179656 | tf_op jit(solution)/shard_map/ppermute | solution.py:15
  53.6 0.5 collective-permute-start.9
  54.2 10.0 %collective-permute-done.8 = f32[6,1,128,128]{3,2,1,0:T(8,128)S(1)} collective-permute-done((f32[6,1,128,128]{3,2,1,0:T(8,128)S(1)}, f32[6,1,128,128]{3,2,1,0:T(8,128)S(1)}, u32[]{:S(2)}, u32[]{:S(2)}) %collective-permute-start.8) | collective-permute-done | bytes 393248 | tf_op jit(solution)/shard_map/ppermute | solution.py:15
  64.1 7.6 %collective-permute-done.9 = f32[6,1,128,128]{3,2,1,0:T(8,128)S(1)} collective-permute-done((f32[6,1,128,128]{3,2,1,0:T(8,128)S(1)}, f32[6,1,128,128]{3,2,1,0:T(8,128)S(1)}, u32[]{:S(2)}, u32[]{:S(2)}) %collective-permute-start.9) | collective-permute-done | bytes 393248 | tf_op jit(solution)/shard_map/ppermute | solution.py:18
  71.7 0.1 pad_maximum_fusion.61
  71.8 0.7 collective-permute-start.10
  72.5 1.4 collective-permute-start.11
  73.9 2.1 %collective-permute-done.10 = f32[6,18,1,128]{3,2,1,0:T(1,128)S(1)} collective-permute-done((f32[6,18,1,128]{3,2,1,0:T(1,128)S(1)}, f32[6,18,1,128]{3,2,1,0:T(1,128)S(1)}, u32[]{:S(2)}, u32[]{:S(2)}) %collective-permute-start.10) | collective-permute-done | bytes 55328 | tf_op jit(solution)/shard_map/ppermute | solution.py:15
  76.0 0.6 collective-permute-done.11
  76.6 0.0 copy-done.1
  76.6 7.6 %fusion.13 = f32[4,16,128,128]{3,2,1,0:T(8,128)S(1)} fusion(f32[4,16,128,128]{3,2,1,0:T(8,128)S(1)} %copy-done, f32[4,16,128,128]{3,2,1,0:T(8,128)S(1)} %fusion.22, f32[4,16,128,128]{3,2,1,0:T(8,128)S(1)} %copy-done.1, f32[6,18,1,128]{3,2,1,0:T(1,128)S(1)} %collective-permute-done.11, f32[6,1,128,128]{3,2,1,0:T(8,128)S(1)} %collective-permute-done.9, ...), kind=kLoop, calls=%fused_computation.32 | loop fusion | flops 29360128 | bytes 19771392 | tf_op jit(solution)/shard_map/add | solution.py:40
  84.2 0.2 fusion.30
  84.4 0.1 collective-permute-start.12
  84.5 0.5 collective-permute-start.13
  85.0 2.1 %collective-permute-done.12 = f32[1,16,128,128]{3,2,1,0:T(8,128)S(1)} collective-permute-done((f32[1,16,128,128]{3,2,1,0:T(8,128)S(1)}, f32[1,16,128,128]{3,2,1,0:T(8,128)S(1)}, u32[]{:S(2)}, u32[]{:S(2)}) %collective-permute-start.12) | collective-permute-done | bytes 1048608 | tf_op jit(solution)/shard_map/ppermute | solution.py:15
  87.2 1.5 %collective-permute-done.13 = f32[1,16,128,128]{3,2,1,0:T(8,128)S(1)} collective-permute-done((f32[1,16,128,128]{3,2,1,0:T(8,128)S(1)}, f32[1,16,128,128]{3,2,1,0:T(8,128)S(1)}, u32[]{:S(2)}, u32[]{:S(2)}) %collective-permute-start.13) | collective-permute-done | bytes 1048608 | tf_op jit(solution)/shard_map/ppermute | solution.py:18
  88.7 0.1 pad_maximum_fusion.48
  88.7 1.6 %collective-permute-start.14 = (f32[6,1,128,128]{3,2,1,0:T(8,128)S(1)}, f32[6,1,128,128]{3,2,1,0:T(8,128)S(1)}, u32[]{:S(2)}, u32[]{:S(2)}) collective-permute-start(f32[6,1,128,128]{3,2,1,0:T(8,128)S(1)} %get-tuple-element.10), channel_id=1, source_target_pairs={{0,2},{2,0},{1,3},{3,1},{4,6},{6,4},{5,7},{7,5},{8,10},{10,8},{9,1... | collective-permute-start | bytes 1179656 | tf_op jit(solution)/shard_map/ppermute | solution.py:15
  90.3 0.5 collective-permute-start.15
  90.8 10.0 %collective-permute-done.14 = f32[6,1,128,128]{3,2,1,0:T(8,128)S(1)} collective-permute-done((f32[6,1,128,128]{3,2,1,0:T(8,128)S(1)}, f32[6,1,128,128]{3,2,1,0:T(8,128)S(1)}, u32[]{:S(2)}, u32[]{:S(2)}) %collective-permute-start.14) | collective-permute-done | bytes 393248 | tf_op jit(solution)/shard_map/ppermute | solution.py:15
  100.8 7.6 %collective-permute-done.15 = f32[6,1,128,128]{3,2,1,0:T(8,128)S(1)} collective-permute-done((f32[6,1,128,128]{3,2,1,0:T(8,128)S(1)}, f32[6,1,128,128]{3,2,1,0:T(8,128)S(1)}, u32[]{:S(2)}, u32[]{:S(2)}) %collective-permute-start.15) | collective-permute-done | bytes 393248 | tf_op jit(solution)/shard_map/ppermute | solution.py:18
  108.4 0.1 pad_maximum_fusion.56
  108.4 1.5 %collective-permute-start.16 = (f32[6,18,1,128]{3,2,1,0:T(1,128)S(1)}, f32[6,18,1,128]{3,2,1,0:T(1,128)S(1)}, u32[]{:S(2)}, u32[]{:S(2)}) collective-permute-start(f32[6,18,1,128]{3,2,1,0:T(1,128)S(1)} %get-tuple-element.4), channel_id=1, source_target_pairs={{0,1},{1,0},{2,3},{3,2},{4,5},{5,4},{6,7},{7,6},{8,9},{9,8},{10,11... | collective-permute-start | bytes 165896 | tf_op jit(solution)/shard_map/ppermute | solution.py:15
  109.9 0.6 collective-permute-start.17
  110.5 2.2 %collective-permute-done.16 = f32[6,18,1,128]{3,2,1,0:T(1,128)S(1)} collective-permute-done((f32[6,18,1,128]{3,2,1,0:T(1,128)S(1)}, f32[6,18,1,128]{3,2,1,0:T(1,128)S(1)}, u32[]{:S(2)}, u32[]{:S(2)}) %collective-permute-start.16) | collective-permute-done | bytes 55328 | tf_op jit(solution)/shard_map/ppermute | solution.py:15
  112.7 1.4 collective-permute-done.17
  114.1 9.3 %fusion.27 = (f32[4,16,128]{2,1,0:T(8,128)S(1)}, f32[4,16,128,128]{3,2,1,0:T(8,128)}) fusion(f32[4,16,128,128]{3,2,1,0:T(8,128)S(1)} %copy-done, f32[4,16,128,128]{3,2,1,0:T(8,128)S(1)} %fusion.13, f32[4,16,128,128]{3,2,1,0:T(8,128)S(1)} %copy-done.1, f32[6,18,1,128]{3,2,1,0:T(1,128)S(1)} %collective-permute-done.17, ...), kind=kLoop, calls=%fused_computation.99 | loop fusion | flops 30400512 | bytes 19804160 | tf_op jit(solution)/shard_map/reduce_sum | solution.py:48
  123.4 7.4 %psum.7 = f32[4,16,1,128]{3,1,0,2:T(8,128)S(1)} all-reduce(f32[4,16,1,128]{3,1,0,2:T(8,128)S(1)} %bitcast.5), channel_id=1, replica_groups=mesh['trial'=4,'south'=2,'east'=2,'down'=2] {'down'}, use_global_device_ids=true, to_apply=%region_1.0 | all-reduce | flops 8192 | bytes 65536 | tf_op jit(solution)/shard_map/psum | solution.py:48
  130.8 3.0 %multiply_reduce_fusion = f32[4,16,128]{2,1,0:T(8,128)S(1)} fusion(f32[4,16,128,128]{3,2,1,0:T(8,128)} %get-tuple-element.3, f32[4,16,128]{2,1,0:T(8,128)S(1)} %multiply_bitcast_fusion), kind=kLoop, calls=%fused_computation.73 | loop fusion | flops 3137536 | bytes 4259840 | tf_op jit(solution)/shard_map/reduce_sum | solution.py:51
  133.8 4.6 %all-gather = f32[8,16,128]{2,1,0:T(8,128)S(1)} all-gather(f32[4,16,128]{2,1,0:T(8,128)S(1)} %multiply_reduce_fusion), channel_id=2, replica_groups=mesh['trial'=4,'south'=2,'east'=2,'down'=2] {'down'}, dimensions={0}, use_global_device_ids=true | all-gather | bytes 98304 | tf_op jit(solution)/shard_map/all_gather | solution.py:51
  138.4 5.2 %subtract_multiply_fusion = f32[4,16,128,128]{3,2,1,0:T(8,128)} fusion(f32[4,16,128,128]{3,2,1,0:T(8,128)} %get-tuple-element.3, f32[4,16,128]{2,1,0:T(8,128)S(1)} %add_rsqrt_fusion, f32[4,16,128]{2,1,0:T(8,128)S(1)} %multiply_bitcast_fusion), kind=kLoop, calls=%fused_computation.74 | loop fusion | flops 2097152 | bytes 8454144 | tf_op jit(solution)/shard_map/mul | solution.py:54
  (3 shorter events, 0.0 us)
Async XLA Ops:
  0.6 4.8 %copy-start.3 = (f32[4,16,128,128]{3,2,1,0:T(8,128)S(1)}, f32[4,16,128,128]{3,2,1,0:T(8,128)}, u32[]{:S(2)}) copy-start(f32[4,16,128,128]{3,2,1,0:T(8,128)} %param.3) | copy-start | bytes 12582916
  2.5 2.8 %collective-permute-start = (f32[1,16,128,128]{3,2,1,0:T(8,128)S(1)}, f32[1,16,128,128]{3,2,1,0:T(8,128)S(1)}, u32[]{:S(2)}, u32[]{:S(2)}) collective-permute-start(f32[1,16,128,128]{3,2,1,0:T(8,128)S(1)} %get-tuple-element.21), channel_id=1, source_target_pairs={{0,4},{4,0},{1,5},{5,1},{2,6},{6,2},{3,7},{7,3},{8,12},{12,8},{9,1... | collective-permute-start | bytes 3145736 | tf_op jit(solution)/shard_map/ppermute | solution.py:15
  3.0 3.8 %collective-permute-start.1 = (f32[1,16,128,128]{3,2,1,0:T(8,128)S(1)}, f32[1,16,128,128]{3,2,1,0:T(8,128)S(1)}, u32[]{:S(2)}, u32[]{:S(2)}) collective-permute-start(f32[1,16,128,128]{3,2,1,0:T(8,128)S(1)} %get-tuple-element.20), channel_id=1, source_target_pairs={{4,0},{0,4},{5,1},{1,5},{6,2},{2,6},{7,3},{3,7},{12,8},{8,12},{13,... | collective-permute-start | bytes 3145736 | tf_op jit(solution)/shard_map/ppermute | solution.py:18
  6.9 25.5 %copy-start.2 = (f32[6,16,128,128]{3,2,1,0:T(8,128)}, f32[6,16,128,128]{3,2,1,0:T(8,128)S(1)}, u32[]{:S(2)}) copy-start(f32[6,16,128,128]{3,2,1,0:T(8,128)S(1)} %constant_dynamic-update-slice_fusion) | copy-start | bytes 18874372
  6.9 26.9 %copy-start = (f32[4,16,128,128]{3,2,1,0:T(8,128)S(1)}, f32[4,16,128,128]{3,2,1,0:T(8,128)}, u32[]{:S(2)}) copy-start(f32[4,16,128,128]{3,2,1,0:T(8,128)} %param.5) | copy-start | bytes 12582916
  7.0 12.9 %collective-permute-start.2 = (f32[6,1,128,128]{3,2,1,0:T(8,128)S(1)}, f32[6,1,128,128]{3,2,1,0:T(8,128)S(1)}, u32[]{:S(2)}, u32[]{:S(2)}) collective-permute-start(f32[6,1,128,128]{3,2,1,0:T(8,128)S(1)} %get-tuple-element.14), channel_id=1, source_target_pairs={{0,2},{2,0},{1,3},{3,1},{4,6},{6,4},{5,7},{7,5},{8,10},{10,8},{9,1... | collective-permute-start | bytes 1179656 | tf_op jit(solution)/shard_map/ppermute | solution.py:15
  9.9 17.8 %collective-permute-start.3 = (f32[6,1,128,128]{3,2,1,0:T(8,128)S(1)}, f32[6,1,128,128]{3,2,1,0:T(8,128)S(1)}, u32[]{:S(2)}, u32[]{:S(2)}) collective-permute-start(f32[6,1,128,128]{3,2,1,0:T(8,128)S(1)} %get-tuple-element.15), channel_id=1, source_target_pairs={{2,0},{0,2},{3,1},{1,3},{6,4},{4,6},{7,5},{5,7},{10,8},{8,10},{11,... | collective-permute-start | bytes 1179656 | tf_op jit(solution)/shard_map/ppermute | solution.py:18
  27.9 4.6 %collective-permute-start.4 = (f32[6,18,1,128]{3,2,1,0:T(1,128)S(1)}, f32[6,18,1,128]{3,2,1,0:T(1,128)S(1)}, u32[]{:S(2)}, u32[]{:S(2)}) collective-permute-start(f32[6,18,1,128]{3,2,1,0:T(1,128)S(1)} %get-tuple-element.8), channel_id=1, source_target_pairs={{0,1},{1,0},{2,3},{3,2},{4,5},{5,4},{6,7},{7,6},{8,9},{9,8},{10,11... | collective-permute-start | bytes 165896 | tf_op jit(solution)/shard_map/ppermute | solution.py:15
  29.7 4.2 %collective-permute-start.5 = (f32[6,18,1,128]{3,2,1,0:T(1,128)S(1)}, f32[6,18,1,128]{3,2,1,0:T(1,128)S(1)}, u32[]{:S(2)}, u32[]{:S(2)}) collective-permute-start(f32[6,18,1,128]{3,2,1,0:T(1,128)S(1)} %get-tuple-element.9), channel_id=1, source_target_pairs={{1,0},{0,1},{3,2},{2,3},{5,4},{4,5},{7,6},{6,7},{9,8},{8,9},{11,10... | collective-permute-start | bytes 165896 | tf_op jit(solution)/shard_map/ppermute | solution.py:18
  47.8 2.7 %collective-permute-start.6 = (f32[1,16,128,128]{3,2,1,0:T(8,128)S(1)}, f32[1,16,128,128]{3,2,1,0:T(8,128)S(1)}, u32[]{:S(2)}, u32[]{:S(2)}) collective-permute-start(f32[1,16,128,128]{3,2,1,0:T(8,128)S(1)} %get-tuple-element.18), channel_id=1, source_target_pairs={{0,4},{4,0},{1,5},{5,1},{2,6},{6,2},{3,7},{7,3},{8,12},{12,8},{9,1... | collective-permute-start | bytes 3145736 | tf_op jit(solution)/shard_map/ppermute | solution.py:15
  47.8 4.1 %collective-permute-start.7 = (f32[1,16,128,128]{3,2,1,0:T(8,128)S(1)}, f32[1,16,128,128]{3,2,1,0:T(8,128)S(1)}, u32[]{:S(2)}, u32[]{:S(2)}) collective-permute-start(f32[1,16,128,128]{3,2,1,0:T(8,128)S(1)} %get-tuple-element.19), channel_id=1, source_target_pairs={{4,0},{0,4},{5,1},{1,5},{6,2},{2,6},{7,3},{3,7},{12,8},{8,12},{13,... | collective-permute-start | bytes 3145736 | tf_op jit(solution)/shard_map/ppermute | solution.py:18
  52.1 24.6 %copy-start.1 = (f32[4,16,128,128]{3,2,1,0:T(8,128)S(1)}, f32[4,16,128,128]{3,2,1,0:T(8,128)}, u32[]{:S(2)}) copy-start(f32[4,16,128,128]{3,2,1,0:T(8,128)} %param.4) | copy-start | bytes 12582916
  52.1 12.1 %collective-permute-start.8 = (f32[6,1,128,128]{3,2,1,0:T(8,128)S(1)}, f32[6,1,128,128]{3,2,1,0:T(8,128)S(1)}, u32[]{:S(2)}, u32[]{:S(2)}) collective-permute-start(f32[6,1,128,128]{3,2,1,0:T(8,128)S(1)} %get-tuple-element.12), channel_id=1, source_target_pairs={{0,2},{2,0},{1,3},{3,1},{4,6},{6,4},{5,7},{7,5},{8,10},{10,8},{9,1... | collective-permute-start | bytes 1179656 | tf_op jit(solution)/shard_map/ppermute | solution.py:15
  53.6 18.1 %collective-permute-start.9 = (f32[6,1,128,128]{3,2,1,0:T(8,128)S(1)}, f32[6,1,128,128]{3,2,1,0:T(8,128)S(1)}, u32[]{:S(2)}, u32[]{:S(2)}) collective-permute-start(f32[6,1,128,128]{3,2,1,0:T(8,128)S(1)} %get-tuple-element.13), channel_id=1, source_target_pairs={{2,0},{0,2},{3,1},{1,3},{6,4},{4,6},{7,5},{5,7},{10,8},{8,10},{11,... | collective-permute-start | bytes 1179656 | tf_op jit(solution)/shard_map/ppermute | solution.py:18
  71.8 4.2 %collective-permute-start.10 = (f32[6,18,1,128]{3,2,1,0:T(1,128)S(1)}, f32[6,18,1,128]{3,2,1,0:T(1,128)S(1)}, u32[]{:S(2)}, u32[]{:S(2)}) collective-permute-start(f32[6,18,1,128]{3,2,1,0:T(1,128)S(1)} %get-tuple-element.6), channel_id=1, source_target_pairs={{0,1},{1,0},{2,3},{3,2},{4,5},{5,4},{6,7},{7,6},{8,9},{9,8},{10,11... | collective-permute-start | bytes 165896 | tf_op jit(solution)/shard_map/ppermute | solution.py:15
  72.5 4.2 %collective-permute-start.11 = (f32[6,18,1,128]{3,2,1,0:T(1,128)S(1)}, f32[6,18,1,128]{3,2,1,0:T(1,128)S(1)}, u32[]{:S(2)}, u32[]{:S(2)}) collective-permute-start(f32[6,18,1,128]{3,2,1,0:T(1,128)S(1)} %get-tuple-element.7), channel_id=1, source_target_pairs={{1,0},{0,1},{3,2},{2,3},{5,4},{4,5},{7,6},{6,7},{9,8},{8,9},{11,10... | collective-permute-start | bytes 165896 | tf_op jit(solution)/shard_map/ppermute | solution.py:18
  84.4 2.7 %collective-permute-start.12 = (f32[1,16,128,128]{3,2,1,0:T(8,128)S(1)}, f32[1,16,128,128]{3,2,1,0:T(8,128)S(1)}, u32[]{:S(2)}, u32[]{:S(2)}) collective-permute-start(f32[1,16,128,128]{3,2,1,0:T(8,128)S(1)} %get-tuple-element.16), channel_id=1, source_target_pairs={{0,4},{4,0},{1,5},{5,1},{2,6},{6,2},{3,7},{7,3},{8,12},{12,8},{9,1... | collective-permute-start | bytes 3145736 | tf_op jit(solution)/shard_map/ppermute | solution.py:15
  84.5 4.1 %collective-permute-start.13 = (f32[1,16,128,128]{3,2,1,0:T(8,128)S(1)}, f32[1,16,128,128]{3,2,1,0:T(8,128)S(1)}, u32[]{:S(2)}, u32[]{:S(2)}) collective-permute-start(f32[1,16,128,128]{3,2,1,0:T(8,128)S(1)} %get-tuple-element.17), channel_id=1, source_target_pairs={{4,0},{0,4},{5,1},{1,5},{6,2},{2,6},{7,3},{3,7},{12,8},{8,12},{13,... | collective-permute-start | bytes 3145736 | tf_op jit(solution)/shard_map/ppermute | solution.py:18
  88.7 12.1 %collective-permute-start.14 = (f32[6,1,128,128]{3,2,1,0:T(8,128)S(1)}, f32[6,1,128,128]{3,2,1,0:T(8,128)S(1)}, u32[]{:S(2)}, u32[]{:S(2)}) collective-permute-start(f32[6,1,128,128]{3,2,1,0:T(8,128)S(1)} %get-tuple-element.10), channel_id=1, source_target_pairs={{0,2},{2,0},{1,3},{3,1},{4,6},{6,4},{5,7},{7,5},{8,10},{10,8},{9,1... | collective-permute-start | bytes 1179656 | tf_op jit(solution)/shard_map/ppermute | solution.py:15
  90.3 18.1 %collective-permute-start.15 = (f32[6,1,128,128]{3,2,1,0:T(8,128)S(1)}, f32[6,1,128,128]{3,2,1,0:T(8,128)S(1)}, u32[]{:S(2)}, u32[]{:S(2)}) collective-permute-start(f32[6,1,128,128]{3,2,1,0:T(8,128)S(1)} %get-tuple-element.11), channel_id=1, source_target_pairs={{2,0},{0,2},{3,1},{1,3},{6,4},{4,6},{7,5},{5,7},{10,8},{8,10},{11,... | collective-permute-start | bytes 1179656 | tf_op jit(solution)/shard_map/ppermute | solution.py:18
  108.4 4.3 %collective-permute-start.16 = (f32[6,18,1,128]{3,2,1,0:T(1,128)S(1)}, f32[6,18,1,128]{3,2,1,0:T(1,128)S(1)}, u32[]{:S(2)}, u32[]{:S(2)}) collective-permute-start(f32[6,18,1,128]{3,2,1,0:T(1,128)S(1)} %get-tuple-element.4), channel_id=1, source_target_pairs={{0,1},{1,0},{2,3},{3,2},{4,5},{5,4},{6,7},{7,6},{8,9},{9,8},{10,11... | collective-permute-start | bytes 165896 | tf_op jit(solution)/shard_map/ppermute | solution.py:15
  109.9 4.2 %collective-permute-start.17 = (f32[6,18,1,128]{3,2,1,0:T(1,128)S(1)}, f32[6,18,1,128]{3,2,1,0:T(1,128)S(1)}, u32[]{:S(2)}, u32[]{:S(2)}) collective-permute-start(f32[6,18,1,128]{3,2,1,0:T(1,128)S(1)} %get-tuple-element.5), channel_id=1, source_target_pairs={{1,0},{0,1},{3,2},{2,3},{5,4},{4,5},{7,6},{6,7},{9,8},{8,9},{11,10... | collective-permute-start | bytes 165896 | tf_op jit(solution)/shard_map/ppermute | solution.py:18
